TPU v7x, 32 devices: a whole 2x2x4 slice. The times are simulated.
32 devices in a mesh: owner: 4 (over x, core), rows: 8 (over z, y).
Axes of the slice: x: 2, y: 2, z: 4, core: 2. Of those that a mesh axis runs over, the one named last changes fastest.
Arguments:
- w_down: float32 [16, 6400, 4096], P('owner', None, 'rows'), may hold values from -0.109375 to 0.109375
- avg_down: bfloat16 [16, 6400, 4096], P('owner', None, 'rows'), may hold values from -0.0390625 to 0.0390625
- router_weight: float32 [4096, 16], P('rows', 'owner'), may hold values from -0.09375 to 0.09375
- router_gain: float32 [4096], P('rows'), may hold values from 0.25 to 1.75
Outputs:
- serve_down: bfloat16 [16, 6400, 4096], P('owner', 'rows')
- scale_down: float32 [16, 6400], P('owner', 'rows')
- serve_router: bfloat16 [4096, 16], replicated
All inputs are finite; a program needn't handle non-finite values. Where the computation divides by a largest or mean magnitude, that divisor is 1e-20 or more.
Results may differ from a plain program's by a relative error of at most 0.001.
Values may be sent and summed in bfloat16 or wider, within the bound.
A program may use at most 256 MiB of HBM per device.

v0:
```python
import jax
import jax.numpy as jnp
from jax import lax
from jax.sharding import PartitionSpec as P

D_MODEL = 4096


def per_device(w_down, avg_down, router_weight, router_gain):
    fresh_down = w_down + avg_down.astype(jnp.float32)
    total_down = lax.psum(jnp.sum(jnp.abs(fresh_down), axis=2), "rows")
    scale_down = total_down / D_MODEL
    narrow_down = (fresh_down / jnp.expand_dims(scale_down, 2)).astype(jnp.bfloat16)
    serve_down = lax.all_to_all(narrow_down, "rows", split_axis=1, concat_axis=2, tiled=True)
    scale_down = lax.dynamic_slice_in_dim(
        scale_down, lax.axis_index("rows") * serve_down.shape[1], serve_down.shape[1], axis=1
    )
    part_router = (router_weight * router_gain[:, None]).astype(jnp.bfloat16)
    row_router = lax.all_gather(part_router, "rows", axis=0, tiled=True)
    serve_router = lax.all_gather(row_router, "owner", axis=1, tiled=True)
    return (serve_down, scale_down, serve_router)


def solution(mesh):
    return jax.shard_map(
        per_device,
        mesh=mesh,
        in_specs=(
            P("owner", None, "rows"),
            P("owner", None, "rows"),
            P("rows", "owner"),
            P("rows"),
        ),
        out_specs=(P("owner", "rows", None), P("owner", "rows"), P()),
        check_vma=False,
    )
```

profile of v0, /device:TPU:0, one launch (start us, length us, event | category | flops | bytes accessed | tf_op | source)
XLA Modules:
  0.0 904.8 jit_solution(12173530837485246061)
XLA Ops:
  7.2 0.0 all-reduce.2.cloned.1.call-start
  7.2 24.2 %abs_reduce_fusion = f32[4,6400]{1,0:T(4,128)S(1)} fusion(f32[4,6400,512]{2,1,0:T(8,128)} %param.4, bf16[4,6400,512]{2,1,0:T(8,128)(2,1)} %param.5), kind=kLoop, calls=%fused_computation.1 | loop fusion | flops 52403200 | bytes 78745600 | tf_op jit(solution)/shard_map/reduce_sum | solution.py:11
  31.4 2.3 copy.21
  33.7 0.0 all-reduce.2.cloned.1.call-update
  33.7 135.4 %all-reduce.2.cloned.1.call-done = f32[4,6400]{0,1:T(8,128)} async-done(((f32[4,6400]{0,1:T(8,128)}), f32[4,6400]{0,1:T(8,128)}) %all-reduce.2.cloned.1.call-update) | async-done | bytes 102416 | tf_op jit(solution)/shard_map/psum | solution.py:11
  169.1 2.1 broadcast_multiply_fusion
  171.3 1.2 copy.17
  172.5 34.3 %divide_convert_fusion = bf16[4,6400,512]{2,1,0:T(8,128)(2,1)} fusion(f32[4,6400,512]{2,1,0:T(8,128)} %param.4, bf16[4,6400,512]{2,1,0:T(8,128)(2,1)} %param.5, f32[4,6400]{1,0:T(4,128)S(1)} %copy.17), kind=kLoop, calls=%fused_computation | loop fusion | flops 52428800 | bytes 104960000 | tf_op jit(solution)/shard_map/convert_element_type | solution.py:13
  206.8 33.4 %copy.18 = bf16[4,6400,512]{2,0,1:T(4,128)(2,1)} copy(bf16[4,6400,512]{2,1,0:T(8,128)(2,1)} %divide_convert_fusion) | data formatting | bytes 52428800 | tf_op jit(solution)/shard_map/convert_element_type | solution.py:13
  240.2 0.0 copy-start
  240.2 0.0 copy-start.1
  240.2 6.6 all-to-all-start
  246.8 0.0 copy-done
  246.9 0.0 copy-done.1
  246.9 585.0 %all_gather.6 = bf16[4096,4]{0,1:T(4,128)(2,1)S(1)} all-gather(bf16[512,4]{0,1:T(4,128)(2,1)S(1)} %multiply_convert_fusion), channel_id=1, replica_groups=mesh['owner'=4,'rows'=8] {'rows'}, dimensions={0}, use_global_device_ids=true | all-gather | bytes 36864 | tf_op jit(solution)/shard_map/all_gather | solution.py:19
  831.9 5.4 all-gather
  837.3 0.7 reshape.9
  838.0 0.8 constant_dynamic-slice_fusion
  838.8 1.8 copy.20
  840.6 0.0 all-to-all-done
  840.6 18.2 %copy.19 = bf16[4,800,8,512]{3,2,1,0:T(8,128)(2,1)} copy(bf16[4,800,8,512]{3,0,1,2:T(4,128)(2,1)} %bitcast.1) | data formatting | bytes 52428800 | tf_op jit(solution)/shard_map/all_to_all | solution.py:14
  858.8 39.2 %all_to_all.16 = bf16[4,800,4096]{2,1,0:T(8,128)(2,1)} reshape(bf16[4,800,8,512]{3,2,1,0:T(8,128)(2,1)} %copy.19) | data formatting | bytes 52428800 | tf_op jit(solution)/shard_map/all_to_all | solution.py:14
  (1 shorter events, 0.0 us)
Async XLA Ops:
  7.2 162.0 %all-reduce.2.cloned.1.call-start = ((), (), s32[]{:S(2)}) async-start(), calls=%async_computation.1 | async-start | bytes 6553600 | tf_op jit(solution)/shard_map/psum | solution.py:11
  240.2 6.7 copy-start
  240.2 6.7 copy-start.1
  240.2 600.4 %all-to-all-start = ((bf16[4,6400,512]{2,0,1:T(4,128)(2,1)}), bf16[4,6400,512]{2,0,1:T(4,128)(2,1)}, u32[]{:S(2)}, u32[]{:S(2)}) async-start(bf16[4,6400,512]{2,0,1:T(4,128)(2,1)} %copy.18), calls=%async_computation | async-start | bytes 52428800 | tf_op jit(solution)/shard_map/all_to_all | solution.py:14
Sparse Core Ops, SparseCore 0:
  33.9 135.2 all-reduce.1
where the time goes:
time: 906 us; the launch traced here: 905 us
  blocking collectives  590 us (65%)
  waiting for transfers between devices  135 us (15%)
  local copies, waits for them, and re-layouts  97.5 us (11%)
  other arithmetic  60.7 us (7%)
  between operations  14.1 us (2%)
    all_gather x1, blocking collectives, per_device(): row_router = lax.all_gather(part_router, 'rows', axis=0, tiled=True)  585 us
    psum x1, waiting for transfers between devices, per_device(): total_down = lax.psum(jnp.sum(jnp.abs(fresh_down), axis=2), 'rows')  135 us
    all_to_all x2, local copies, waits for them, and re-layouts, per_device(): lax.all_to_all(narrow_down, 'rows', split_axis=1, concat_axis=2, tiled=True)  57.4 us
    convert_element_type x1, other arithmetic, per_device(): (fresh_down / jnp.expand_dims(scale_down, 2)).astype(jnp.bfloat16)  34.3 us
    convert_element_type x1, local copies, waits for them, and re-layouts, per_device(): (fresh_down / jnp.expand_dims(scale_down, 2)).astype(jnp.bfloat16)  33.4 us
    reduce_sum x1, other arithmetic, per_device(): total_down = lax.psum(jnp.sum(jnp.abs(fresh_down), axis=2), 'rows')  24.2 us
  transfers between devices with their start and end apart: 2, of which 1 were waited for; matrix products, arithmetic and copies ran while one was open for 0% of the time, Pallas kernels for 0%

commit v1 on v0

--- a/solution.py
+++ b/solution.py
@@ -17,7 +17,8 @@
     )
     part_router = (router_weight * router_gain[:, None]).astype(jnp.bfloat16)
     row_router = lax.all_gather(part_router, "rows", axis=0, tiled=True)
-    serve_router = lax.all_gather(row_router, "owner", axis=1, tiled=True)
+    blocks = lax.all_gather(row_router, "owner")
+    serve_router = jnp.concatenate(blocks, axis=1)
     return (serve_down, scale_down, serve_router)
 
 

time: 906 us -> 906 us (level)
  no operation moved by 1% of the time
where the time goes in v1:
time: 906 us; the launch traced here: 905 us
  blocking collectives  590 us (65%)
  waiting for transfers between devices  135 us (15%)
  local copies, waits for them, and re-layouts  97.5 us (11%)
  other arithmetic  60.7 us (7%)
  between operations  14.1 us (2%)
    all_gather x1, blocking collectives, per_device(): row_router = lax.all_gather(part_router, 'rows', axis=0, tiled=True)  585 us
    psum x1, waiting for transfers between devices, per_device(): total_down = lax.psum(jnp.sum(jnp.abs(fresh_down), axis=2), 'rows')  135 us
    all_to_all x2, local copies, waits for them, and re-layouts, per_device(): lax.all_to_all(narrow_down, 'rows', split_axis=1, concat_axis=2, tiled=True)  57.4 us
    convert_element_type x1, other arithmetic, per_device(): (fresh_down / jnp.expand_dims(scale_down, 2)).astype(jnp.bfloat16)  34.3 us
    convert_element_type x1, local copies, waits for them, and re-layouts, per_device(): (fresh_down / jnp.expand_dims(scale_down, 2)).astype(jnp.bfloat16)  33.4 us
    reduce_sum x1, other arithmetic, per_device(): total_down = lax.psum(jnp.sum(jnp.abs(fresh_down), axis=2), 'rows')  24.2 us
  transfers between devices with their start and end apart: 2, of which 1 were waited for; matrix products, arithmetic and copies ran while one was open for 0% of the time, Pallas kernels for 0%

profile of v1, /device:TPU:0, one launch (start us, length us, event | category | flops | bytes accessed | tf_op | source)
XLA Modules:
  0.0 904.8 jit_solution(7164546433078577317)
XLA Ops:
  7.2 0.0 all-reduce.2.cloned.1.call-start
  7.2 24.2 %abs_reduce_fusion = f32[4,6400]{1,0:T(4,128)S(1)} fusion(f32[4,6400,512]{2,1,0:T(8,128)} %param.4, bf16[4,6400,512]{2,1,0:T(8,128)(2,1)} %param.5), kind=kLoop, calls=%fused_computation.1 | loop fusion | flops 52403200 | bytes 78745600 | tf_op jit(solution)/shard_map/reduce_sum | solution.py:11
  31.4 2.3 copy.25
  33.7 0.0 all-reduce.2.cloned.1.call-update
  33.7 135.4 %all-reduce.2.cloned.1.call-done = f32[4,6400]{0,1:T(8,128)} async-done(((f32[4,6400]{0,1:T(8,128)}), f32[4,6400]{0,1:T(8,128)}) %all-reduce.2.cloned.1.call-update) | async-done | bytes 102416 | tf_op jit(solution)/shard_map/psum | solution.py:11
  169.1 2.1 broadcast_multiply_fusion
  171.3 1.2 copy.20
  172.5 34.3 %divide_convert_fusion = bf16[4,6400,512]{2,1,0:T(8,128)(2,1)} fusion(f32[4,6400,512]{2,1,0:T(8,128)} %param.4, bf16[4,6400,512]{2,1,0:T(8,128)(2,1)} %param.5, f32[4,6400]{1,0:T(4,128)S(1)} %copy.20), kind=kLoop, calls=%fused_computation | loop fusion | flops 52428800 | bytes 104960000 | tf_op jit(solution)/shard_map/convert_element_type | solution.py:13
  206.8 33.4 %copy.21 = bf16[4,6400,512]{2,0,1:T(4,128)(2,1)} copy(bf16[4,6400,512]{2,1,0:T(8,128)(2,1)} %divide_convert_fusion) | data formatting | bytes 52428800 | tf_op jit(solution)/shard_map/convert_element_type | solution.py:13
  240.2 0.0 copy-start
  240.2 0.0 copy-start.1
  240.2 6.6 all-to-all-start
  246.8 0.0 copy-done
  246.9 0.0 copy-done.1
  246.9 585.0 %all_gather.9 = bf16[4096,4]{0,1:T(4,128)(2,1)S(1)} all-gather(bf16[512,4]{0,1:T(4,128)(2,1)S(1)} %multiply_convert_fusion), channel_id=1, replica_groups=mesh['owner'=4,'rows'=8] {'rows'}, dimensions={0}, use_global_device_ids=true | all-gather | bytes 36864 | tf_op jit(solution)/shard_map/all_gather | solution.py:19
  831.9 5.4 all-gather
  837.3 0.7 reshape.15
  838.0 0.8 constant_dynamic-slice_fusion
  838.8 1.8 copy.24
  840.6 0.0 all-to-all-done
  840.6 18.2 %copy.22 = bf16[4,800,8,512]{3,2,1,0:T(8,128)(2,1)} copy(bf16[4,800,8,512]{3,0,1,2:T(4,128)(2,1)} %bitcast.1) | data formatting | bytes 52428800 | tf_op jit(solution)/shard_map/all_to_all | solution.py:14
  858.8 39.2 %all_to_all.16 = bf16[4,800,4096]{2,1,0:T(8,128)(2,1)} reshape(bf16[4,800,8,512]{3,2,1,0:T(8,128)(2,1)} %copy.22) | data formatting | bytes 52428800 | tf_op jit(solution)/shard_map/all_to_all | solution.py:14
  (1 shorter events, 0.0 us)
Async XLA Ops:
  7.2 162.0 %all-reduce.2.cloned.1.call-start = ((), (), s32[]{:S(2)}) async-start(), calls=%async_computation.1 | async-start | bytes 6553600 | tf_op jit(solution)/shard_map/psum | solution.py:11
  240.2 6.7 copy-start
  240.2 6.7 copy-start.1
  240.2 600.4 %all-to-all-start = ((bf16[4,6400,512]{2,0,1:T(4,128)(2,1)}), bf16[4,6400,512]{2,0,1:T(4,128)(2,1)}, u32[]{:S(2)}, u32[]{:S(2)}) async-start(bf16[4,6400,512]{2,0,1:T(4,128)(2,1)} %copy.21), calls=%async_computation | async-start | bytes 52428800 | tf_op jit(solution)/shard_map/all_to_all | solution.py:14
Sparse Core Ops, SparseCore 0:
  33.9 135.2 all-reduce.1

commit v2 on v0

--- a/solution.py
+++ b/solution.py
@@ -8,7 +8,9 @@
 
 def per_device(w_down, avg_down, router_weight, router_gain):
     fresh_down = w_down + avg_down.astype(jnp.float32)
-    total_down = lax.psum(jnp.sum(jnp.abs(fresh_down), axis=2), "rows")
+    x = jnp.sum(jnp.abs(fresh_down), axis=2)
+    terms = lax.all_gather(x, "rows")
+    total_down = jnp.sum(terms, axis=0)
     scale_down = total_down / D_MODEL
     narrow_down = (fresh_down / jnp.expand_dims(scale_down, 2)).astype(jnp.bfloat16)
     serve_down = lax.all_to_all(narrow_down, "rows", split_axis=1, concat_axis=2, tiled=True)

time: 906 us -> 781 us (0.86)
  waiting for transfers between devices: 135 us -> 0.01 us
  blocking collectives: 590 us -> 620 us
  between operations: 14.1 us -> 0.71 us
    psum x1 -> x0, waiting for transfers between devices: 135 us -> none  [per_device(): total_down = lax.psum(jnp.sum(jnp.abs(fresh_down), axis=2), 'rows')]
    all_gather x0 -> x1, blocking collectives: none -> 33.9 us  [per_device(): terms = lax.all_gather(x, 'rows')]
    reduce_sum x1 -> x2, other arithmetic: 24.2 us -> 24.4 us  [the longest x1 24.2 us: per_device(): x = jnp.sum(jnp.abs(fresh_down), axis=2)]
  transfers between devices with their start and end apart: 2 -> 1, of which waited for: 1 -> 0; matrix products, arithmetic and copies ran while one was open for 0% -> 0% of each run, Pallas kernels for 0% -> 0%
where the time goes in v2:
time: 781 us; the launch traced here: 780 us
  blocking collectives  620 us (79%)
  local copies, waits for them, and re-layouts  94.5 us (12%)
  other arithmetic  58.7 us (8%)
    all_gather x1, blocking collectives, per_device(): row_router = lax.all_gather(part_router, 'rows', axis=0, tiled=True)  580 us
    all_to_all x2, local copies, waits for them, and re-layouts, per_device(): lax.all_to_all(narrow_down, 'rows', split_axis=1, concat_axis=2, tiled=True)  57.4 us
    convert_element_type x1, other arithmetic, per_device(): (fresh_down / jnp.expand_dims(scale_down, 2)).astype(jnp.bfloat16)  34.3 us
    all_gather x1, blocking collectives, per_device(): terms = lax.all_gather(x, 'rows')  33.9 us
    convert_element_type x1, local copies, waits for them, and re-layouts, per_device(): (fresh_down / jnp.expand_dims(scale_down, 2)).astype(jnp.bfloat16)  33.4 us
    reduce_sum x1, other arithmetic, per_device(): x = jnp.sum(jnp.abs(fresh_down), axis=2)  24.2 us
  transfers between devices with their start and end apart: 1, of which 0 were waited for; matrix products, arithmetic and copies ran while one was open for 0% of the time, Pallas kernels for 0%

profile of v2, /device:TPU:0, one launch (start us, length us, event | category | flops | bytes accessed | tf_op | source)
XLA Modules:
  0.0 780.0 jit_solution(4935870876903753817)
XLA Ops:
  0.6 24.2 %abs_reduce_fusion = f32[4,6400]{1,0:T(4,128)S(1)} fusion(f32[4,6400,512]{2,1,0:T(8,128)} %param.4, bf16[4,6400,512]{2,1,0:T(8,128)(2,1)} %param.5), kind=kLoop, calls=%fused_computation.1 | loop fusion | flops 52403200 | bytes 78745600 | tf_op jit(solution)/shard_map/reduce_sum | solution.py:11
  24.9 1.1 copy.21
  26.0 1.2 copy.18
  27.2 33.9 %all-gather.1 = f32[8,4,6400]{2,1,0:T(4,128)S(1)} all-gather(f32[1,4,6400]{2,1,0:T(4,128)S(1)} %copy.18), channel_id=2, replica_groups=mesh['owner'=4,'rows'=8] {'rows'}, dimensions={0}, use_global_device_ids=true | all-gather | bytes 921600 | tf_op jit(solution)/shard_map/all_gather | solution.py:12
  61.2 0.1 reduce_sum.19
  61.3 34.3 %divide_convert_fusion = bf16[4,6400,512]{2,1,0:T(8,128)(2,1)} fusion(f32[4,6400,512]{2,1,0:T(8,128)} %param.4, bf16[4,6400,512]{2,1,0:T(8,128)(2,1)} %param.5, f32[4,6400]{1,0:T(4,128)S(1)} %broadcast_multiply_fusion), kind=kLoop, calls=%fused_computation | loop fusion | flops 52428800 | bytes 104960000 | tf_op jit(solution)/shard_map/convert_element_type | solution.py:15
  95.6 0.0 copy-start
  95.6 0.0 copy-start.1
  95.6 33.4 %copy.19 = bf16[4,6400,512]{2,0,1:T(4,128)(2,1)} copy(bf16[4,6400,512]{2,1,0:T(8,128)(2,1)} %divide_convert_fusion) | data formatting | bytes 52428800 | tf_op jit(solution)/shard_map/convert_element_type | solution.py:15
  129.0 6.5 all-to-all-start
  135.5 0.0 copy-done
  135.5 0.0 copy-done.1
  135.6 580.3 %all_gather.14 = bf16[4096,4]{0,1:T(4,128)(2,1)S(1)} all-gather(bf16[512,4]{0,1:T(4,128)(2,1)S(1)} %multiply_convert_fusion), channel_id=1, replica_groups=mesh['owner'=4,'rows'=8] {'rows'}, dimensions={0}, use_global_device_ids=true | all-gather | bytes 36864 | tf_op jit(solution)/shard_map/all_gather | solution.py:21
  715.8 5.4 all-gather.2
  721.2 0.7 reshape.14
  721.9 0.7 constant_dynamic-slice_fusion
  722.6 0.0 all-to-all-done
  722.6 18.2 %copy.20 = bf16[4,800,8,512]{3,2,1,0:T(8,128)(2,1)} copy(bf16[4,800,8,512]{3,0,1,2:T(4,128)(2,1)} %bitcast.2) | data formatting | bytes 52428800 | tf_op jit(solution)/shard_map/all_to_all | solution.py:16
  740.8 39.2 %all_to_all.16 = bf16[4,800,4096]{2,1,0:T(8,128)(2,1)} reshape(bf16[4,800,8,512]{3,2,1,0:T(8,128)(2,1)} %copy.20) | data formatting | bytes 52428800 | tf_op jit(solution)/shard_map/all_to_all | solution.py:16
  (2 shorter events, 0.0 us)
Async XLA Ops:
  95.6 39.9 %copy-start = (f32[512,4]{0,1:T(4,128)S(1)}, f32[512,4]{0,1:T(4,128)}, u32[]{:S(2)}) copy-start(f32[512,4]{0,1:T(4,128)} %param.6) | copy-start | bytes 24580
  95.6 39.9 %copy-start.1 = (f32[512]{0:T(512)S(1)}, f32[512]{0:T(512)}, u32[]{:S(2)}) copy-start(f32[512]{0:T(512)} %param.7) | copy-start | bytes 6148
  129.0 593.6 %all-to-all-start = ((bf16[4,6400,512]{2,0,1:T(4,128)(2,1)}), bf16[4,6400,512]{2,0,1:T(4,128)(2,1)}, u32[]{:S(2)}, u32[]{:S(2)}) async-start(bf16[4,6400,512]{2,0,1:T(4,128)(2,1)} %copy.19), calls=%async_computation | async-start | bytes 52428800 | tf_op jit(solution)/shard_map/all_to_all | solution.py:16

commit v3 on v0

--- a/solution.py
+++ b/solution.py
@@ -11,7 +11,10 @@
     total_down = lax.psum(jnp.sum(jnp.abs(fresh_down), axis=2), "rows")
     scale_down = total_down / D_MODEL
     narrow_down = (fresh_down / jnp.expand_dims(scale_down, 2)).astype(jnp.bfloat16)
-    serve_down = lax.all_to_all(narrow_down, "rows", split_axis=1, concat_axis=2, tiled=True)
+    size = lax.axis_size("rows")
+    pieces = jnp.stack(jnp.split(narrow_down, size, axis=1), axis=0)
+    pieces = lax.all_to_all(pieces, "rows", split_axis=0, concat_axis=0)
+    serve_down = jnp.concatenate(pieces, axis=2)
     scale_down = lax.dynamic_slice_in_dim(
         scale_down, lax.axis_index("rows") * serve_down.shape[1], serve_down.shape[1], axis=1
     )

time: 906 us -> 792 us (0.87)
  waiting for transfers between devices: 135 us -> 72.4 us
  local copies, waits for them, and re-layouts: 97.5 us -> 49.9 us
    psum x1, waiting for transfers between devices: 135 us -> 72.4 us  [per_device(): total_down = lax.psum(jnp.sum(jnp.abs(fresh_down), axis=2), 'rows')]
    all_to_all x2 -> x0, local copies, waits for them, and re-layouts: 57.4 us -> none  [per_device(): lax.all_to_all(narrow_down, 'rows', split_axis=1, concat_axis=2, tiled=True)]
    convert_element_type x1 -> x0, local copies, waits for them, and re-layouts: 33.4 us -> none  [per_device(): (fresh_down / jnp.expand_dims(scale_down, 2)).astype(jnp.bfloat16)]
    unnamed x7 -> x12, local copies, waits for them, and re-layouts: 4.74 us -> 27.5 us
    reshape x0 -> x1, local copies, waits for them, and re-layouts: none -> 17.9 us  [per_device(): serve_down = jnp.concatenate(pieces, axis=2)]
where the time goes in v3:
time: 792 us
  blocking collectives  589 us (74%)
  waiting for transfers between devices  72.4 us (9%)
  other arithmetic  60.1 us (8%)
  local copies, waits for them, and re-layouts  49.9 us (6%)
  between operations  14.1 us (2%)
    all_gather x1, blocking collectives, per_device(): row_router = lax.all_gather(part_router, 'rows', axis=0, tiled=True)  583 us
    psum x1, waiting for transfers between devices, per_device(): total_down = lax.psum(jnp.sum(jnp.abs(fresh_down), axis=2), 'rows')  72.4 us
    convert_element_type x1, other arithmetic, per_device(): (fresh_down / jnp.expand_dims(scale_down, 2)).astype(jnp.bfloat16)  34.3 us
    unnamed x12, local copies, waits for them, and re-layouts  27.5 us
    reduce_sum x1, other arithmetic, per_device(): total_down = lax.psum(jnp.sum(jnp.abs(fresh_down), axis=2), 'rows')  24.9 us
    reshape x1, local copies, waits for them, and re-layouts, per_device(): serve_down = jnp.concatenate(pieces, axis=2)  17.9 us
  transfers between devices with their start and end apart: 2, of which 1 were waited for; matrix products, arithmetic and copies ran while one was open for 0% of the time, Pallas kernels for 0%

profile of v3, /device:TPU:0, one launch (start us, length us, event | category | flops | bytes accessed | tf_op | source)
XLA Modules:
  0.0 791.9 jit_solution(5396997361598960320)
XLA Ops:
  7.2 0.0 all-reduce.2.cloned.1.call-start
  7.2 24.9 %abs_reduce_fusion = f32[4,6400]{1,0:T(4,128)} fusion(f32[4,6400,512]{2,1,0:T(8,128)} %param.4, bf16[4,6400,512]{2,1,0:T(8,128)(2,1)} %param.5), kind=kLoop, calls=%fused_computation.1 | loop fusion | flops 52403200 | bytes 78745600 | tf_op jit(solution)/shard_map/reduce_sum | solution.py:11
  32.1 0.0 all-reduce.2.cloned.1.call-update
  32.1 72.4 %all-reduce.2.cloned.1.call-done = f32[4,6400]{1,0:T(4,128)} async-done(((f32[4,6400]{1,0:T(4,128)}), f32[4,6400]{1,0:T(4,128)}) %all-reduce.2.cloned.1.call-update) | async-done | bytes 102416 | tf_op jit(solution)/shard_map/psum | solution.py:11
  104.5 0.9 broadcast_multiply_fusion
  105.4 34.3 %divide_convert_fusion = bf16[4,6400,512]{2,1,0:T(8,128)(2,1)} fusion(f32[4,6400,512]{2,1,0:T(8,128)} %param.4, bf16[4,6400,512]{2,1,0:T(8,128)(2,1)} %param.5, f32[4,6400]{1,0:T(4,128)S(1)} %broadcast_multiply_fusion), kind=kLoop, calls=%fused_computation | loop fusion | flops 52428800 | bytes 104960000 | tf_op jit(solution)/shard_map/convert_element_type | solution.py:13
  139.7 3.8 fusion.7
  143.5 3.8 fusion.6
  147.4 3.8 fusion.5
  151.2 3.8 fusion.4
  155.0 3.9 fusion.3
  158.9 3.8 fusion.2
  162.7 3.8 fusion.1
  166.5 3.8 fusion
  170.3 0.0 copy-start
  170.3 0.0 copy-start.1
  170.3 6.6 all-to-all-start
  177.0 0.0 copy-done
  177.0 0.0 copy-done.1
  177.0 583.4 %all_gather.6 = bf16[4096,4]{0,1:T(4,128)(2,1)S(1)} all-gather(bf16[512,4]{0,1:T(4,128)(2,1)S(1)} %multiply_convert_fusion), channel_id=1, replica_groups=mesh['owner'=4,'rows'=8] {'rows'}, dimensions={0}, use_global_device_ids=true | all-gather | bytes 36864 | tf_op jit(solution)/shard_map/all_gather | solution.py:22
  760.4 5.4 all-gather
  765.8 0.7 reshape.17
  766.5 0.7 constant_dynamic-slice_fusion
  767.2 0.0 all-to-all-done
  767.2 17.9 %copy.9 = bf16[8,4,100,8,512]{4,3,0,2,1:T(8,128)(2,1)} copy(bf16[8,4,100,8,512]{4,3,2,1,0:T(8,128)(2,1)} %bitcast.13) | data formatting | bytes 52428800 | tf_op jit(solution)/shard_map/reshape | solution.py:17
  (1 shorter events, 0.0 us)
Async XLA Ops:
  7.2 97.3 %all-reduce.2.cloned.1.call-start = ((), (), s32[]{:S(2)}) async-start(), calls=%async_computation.1 | async-start | bytes 204800 | tf_op jit(solution)/shard_map/psum | solution.py:11
  170.3 6.6 copy-start
  170.3 6.6 copy-start.1
  170.3 596.9 %all-to-all-start = ((bf16[8,4,800,512]{3,2,1,0:T(8,128)(2,1)}), bf16[8,4,800,512]{3,2,1,0:T(8,128)(2,1)}, u32[]{:S(2)}, u32[]{:S(2)}) async-start(bf16[8,4,800,512]{3,2,1,0:T(8,128)(2,1)} %fusion), calls=%async_computation | async-start | bytes 52428800 | tf_op jit(solution)/shard_map/all_to_all | solution.py:16
Sparse Core Ops, SparseCore 0:
  32.2 72.2 all-reduce.1
